TPU v7x, 32 devices: a whole 2x2x4 slice. The times are simulated.
32 devices in a mesh: dp: 4 (over y, x), fsdp: 8 (over z, core).
Axes of the slice: x: 2, y: 2, z: 4, core: 2. Of those that a mesh axis runs over, the one named last changes fastest.
Arguments:
- tokens: bfloat16 [32768, 768], P(('dp', 'fsdp')), may hold values from -6 to 6
- cotangent: bfloat16 [32768, 768], P(('dp', 'fsdp')), may hold values from -6 to 6
- lengths: int32 [64], P(('dp', 'fsdp')), may hold values from 128 to 512, as said below
- mb_count: int32 [4], replicated, may hold values from 1 to 2, as said below
- query_weight: bfloat16 [768, 768], P('fsdp'), may hold values from -0.21875 to 0.21875
- query_bias: bfloat16 [768], P('fsdp'), may hold values from -1.5 to 1.5
- key_weight: bfloat16 [768, 768], P('fsdp'), may hold values from -0.21875 to 0.21875
- value_weight: bfloat16 [768, 768], P('fsdp'), may hold values from -0.21875 to 0.21875
- value_bias: bfloat16 [768], P('fsdp'), may hold values from -1.5 to 1.5
- output_weight: bfloat16 [768, 768], P('fsdp'), may hold values from -1.75 to 1.75
- output_bias: bfloat16 [768], P('fsdp'), may hold values from -1.5 to 1.5
- first_gain: bfloat16 [768], P('fsdp'), may hold values from 0.5 to 1.5
- first_shift: bfloat16 [768], P('fsdp'), may hold values from -1.5 to 1.5
- up_weight: bfloat16 [768, 3072], P('fsdp'), may hold values from -0.21875 to 0.21875
- up_bias: bfloat16 [3072], P('fsdp'), may hold values from -1.5 to 1.5
- down_weight: bfloat16 [3072, 768], P('fsdp'), may hold values from -0.109375 to 0.109375
- down_bias: bfloat16 [768], P('fsdp'), may hold values from -1.5 to 1.5
- second_gain: bfloat16 [768], P('fsdp'), may hold values from 0.5 to 1.5
- second_shift: bfloat16 [768], P('fsdp'), may hold values from -1.5 to 1.5
Outputs:
- layer_out: bfloat16 [32768, 768], P(('dp', 'fsdp'))
- tokens_grad: bfloat16 [32768, 768], P(('dp', 'fsdp'))
- query_weight_grad: float32 [768, 768], P('fsdp')
- query_bias_grad: float32 [768], P('fsdp')
- key_weight_grad: float32 [768, 768], P('fsdp')
- value_weight_grad: float32 [768, 768], P('fsdp')
- value_bias_grad: float32 [768], P('fsdp')
- output_weight_grad: float32 [768, 768], P('fsdp')
- output_bias_grad: float32 [768], P('fsdp')
- first_gain_grad: float32 [768], P('fsdp')
- first_shift_grad: float32 [768], P('fsdp')
- up_weight_grad: float32 [768, 3072], P('fsdp')
- up_bias_grad: float32 [3072], P('fsdp')
- down_weight_grad: float32 [3072, 768], P('fsdp')
- down_bias_grad: float32 [768], P('fsdp')
- second_gain_grad: float32 [768], P('fsdp')
- second_shift_grad: float32 [768], P('fsdp')
Inputs may be any that keep to these rules, and one draw needn't show every extreme that they name: `lengths`: keys at positions at or past a sequence's length are padding; some sequence has all 512 keys valid and some has 128. Data group g runs slots 0 .. mb_count[g] - 1 of each of its devices; some group runs all 2 and some runs one.
All inputs are finite; a program needn't handle non-finite values.
Results may differ from a plain program's by a relative error of at most 0.02.
Values may be sent and summed in bfloat16 or wider, within the bound.
A program may use at most 144 MiB of HBM per device.

v0:
```python
import jax
import jax.numpy as jnp
from jax import lax
from jax.sharding import PartitionSpec as P

HEADS = 12
MB_CAP = 2
norm_epsilon = 1e-05


def for_sending(shard):

    def short(part):
        return part.astype(jnp.bfloat16) if part.dtype == jnp.float32 else part

    return jax.tree.map(short, shard)


def gelu_exact(values):
    return jax.nn.gelu(values, approximate=False)


def layer_norm(hidden, gain, shift):
    centre = hidden - jnp.mean(hidden, axis=-1, keepdims=True)
    inverse = lax.rsqrt(jnp.mean(centre * centre, axis=-1, keepdims=True) + norm_epsilon)
    normed = centre * inverse
    return (normed * gain.astype(jnp.float32) + shift.astype(jnp.float32), normed, inverse)


def norm_backward(grad_out, normed, inverse, gain):
    scaled = grad_out * gain.astype(jnp.float32)
    inner = scaled - jnp.mean(scaled, axis=-1, keepdims=True)
    inner = inner - normed * jnp.mean(scaled * normed, axis=-1, keepdims=True)
    return inverse * inner


def to_heads(values, seq_count, heads):
    width = values.shape[1]
    shaped = values.reshape(seq_count, -1, heads, width // heads)
    return jnp.transpose(shaped, (0, 2, 3, 1))


def from_heads(values):
    shaped = jnp.transpose(values, (0, 3, 1, 2))
    return shaped.reshape(-1, values.shape[1] * values.shape[2])


def masked_scores(query_cols, key_cols, length):
    factor = query_cols.shape[1] ** (-0.5)
    scores = (
        jnp.einsum("hdq,hdk->hqk", query_cols, key_cols, preferred_element_type=jnp.float32)
        * factor
    )
    visible = jnp.arange(key_cols.shape[2], dtype=jnp.int32) < length
    masked = jnp.where(visible[None, None, :], scores, -1000000000.0)
    return (masked, factor)


def attend_forward(query_cols, key_cols, value_cols, length):
    scores, factor = masked_scores(query_cols, key_cols, length)
    top = jnp.max(scores, axis=-1, keepdims=True)
    expo = jnp.exp(scores - top)
    total = jnp.sum(expo, axis=-1, keepdims=True)
    probs = (expo / total).astype(jnp.bfloat16)
    log_total = top[..., 0] + jnp.log(total[..., 0])
    context = jnp.einsum("hdk,hqk->hdq", value_cols, probs, preferred_element_type=jnp.float32)
    return (context.astype(jnp.bfloat16), log_total)


def attend_backward(query_cols, key_cols, value_cols, length, log_total, grad_cols):
    scores, factor = masked_scores(query_cols, key_cols, length)
    probs = jnp.exp(scores - log_total[..., None])
    grad_probs = jnp.einsum(
        "hdq,hdk->hqk", grad_cols, value_cols, preferred_element_type=jnp.float32
    )
    grad_values = jnp.einsum(
        "hqk,hdq->hdk", probs.astype(jnp.bfloat16), grad_cols, preferred_element_type=jnp.float32
    ).astype(jnp.bfloat16)
    delta = jnp.sum(grad_probs * probs, axis=-1, keepdims=True)
    grad_scores = (probs * (grad_probs - delta)).astype(jnp.bfloat16)
    grad_queries = (
        factor
        * jnp.einsum("hqk,hdk->hdq", grad_scores, key_cols, preferred_element_type=jnp.float32)
    ).astype(jnp.bfloat16)
    grad_keys = (
        factor
        * jnp.einsum("hqk,hdq->hdk", grad_scores, query_cols, preferred_element_type=jnp.float32)
    ).astype(jnp.bfloat16)
    return (grad_queries, grad_keys, grad_values)


def project(left, right):
    return jnp.dot(left, right, preferred_element_type=jnp.float32)


def project_back(left, right):
    return jnp.einsum("rc,dc->rd", left, right, preferred_element_type=jnp.float32)


def weight_grad(left, right):
    return jnp.einsum("rc,rd->cd", left, right, preferred_element_type=jnp.float32)


def column_sum(values):
    return jnp.sum(values.astype(jnp.float32), axis=0)


def slot_forward(rows, weights, seq_lengths, heads):
    (
        w_query,
        b_query,
        w_key,
        w_value,
        b_value,
        w_output,
        b_output,
        gain_one,
        shift_one,
        w_up,
        b_up,
        w_down,
        b_down,
        gain_two,
        shift_two,
    ) = weights
    seq_count = seq_lengths.shape[0]
    queries = (project(rows, w_query) + b_query.astype(jnp.float32)).astype(jnp.bfloat16)
    key_rows = project(rows, w_key).astype(jnp.bfloat16)
    value_rows = (project(rows, w_value) + b_value.astype(jnp.float32)).astype(jnp.bfloat16)
    query_cols = to_heads(queries, seq_count, heads)
    key_cols = to_heads(key_rows, seq_count, heads)
    value_cols = to_heads(value_rows, seq_count, heads)

    def one_sequence(item):
        return attend_forward(item[0], item[1], item[2], item[3])

    context_cols, log_total = lax.map(one_sequence, (query_cols, key_cols, value_cols, seq_lengths))
    context = from_heads(context_cols)
    first_sum = rows.astype(jnp.float32) + project(context, w_output) + b_output.astype(jnp.float32)
    middle, normed_one, inverse_one = layer_norm(first_sum, gain_one, shift_one)
    middle_low = middle.astype(jnp.bfloat16)
    upper = project(middle_low, w_up) + b_up.astype(jnp.float32)
    active = gelu_exact(upper).astype(jnp.bfloat16)
    second_sum = middle + project(active, w_down) + b_down.astype(jnp.float32)
    result, normed_two, inverse_two = layer_norm(second_sum, gain_two, shift_two)
    saved = (
        query_cols,
        key_cols,
        value_cols,
        log_total,
        context,
        normed_one,
        inverse_one,
        middle_low,
        upper,
        active,
        normed_two,
        inverse_two,
    )
    return (result, saved)


def slot_backward(rows, grad_out, saved, weights, seq_lengths, heads):
    (
        w_query,
        b_query,
        w_key,
        w_value,
        b_value,
        w_output,
        b_output,
        gain_one,
        shift_one,
        w_up,
        b_up,
        w_down,
        b_down,
        gain_two,
        shift_two,
    ) = weights
    (
        query_cols,
        key_cols,
        value_cols,
        log_total,
        context,
        normed_one,
        inverse_one,
        middle_low,
        upper,
        active,
        normed_two,
        inverse_two,
    ) = saved
    seq_count = seq_lengths.shape[0]
    gain_two_grad = jnp.sum(grad_out * normed_two, axis=0)
    shift_two_grad = jnp.sum(grad_out, axis=0)
    grad_second = norm_backward(grad_out, normed_two, inverse_two, gain_two)
    grad_down = grad_second.astype(jnp.bfloat16)
    down_bias_grad = column_sum(grad_down)
    down_weight_grad = weight_grad(active, grad_down)
    grad_active = project_back(grad_down, w_down)
    gelu_value, gelu_pull = jax.vjp(gelu_exact, upper)
    grad_upper = gelu_pull(grad_active)[0].astype(jnp.bfloat16)
    up_bias_grad = column_sum(grad_upper)
    up_weight_grad = weight_grad(middle_low, grad_upper)
    grad_middle = grad_second + project_back(grad_upper, w_up)
    gain_one_grad = jnp.sum(grad_middle * normed_one, axis=0)
    shift_one_grad = jnp.sum(grad_middle, axis=0)
    grad_first = norm_backward(grad_middle, normed_one, inverse_one, gain_one)
    grad_branch = grad_first.astype(jnp.bfloat16)
    output_bias_grad = column_sum(grad_branch)
    output_weight_grad = weight_grad(context, grad_branch)
    grad_context = project_back(grad_branch, w_output).astype(jnp.bfloat16)
    grad_cols = to_heads(grad_context, seq_count, heads)

    def one_sequence(item):
        return attend_backward(item[0], item[1], item[2], item[3], item[4], item[5])

    grad_query_cols, grad_key_cols, grad_value_cols = lax.map(
        one_sequence, (query_cols, key_cols, value_cols, seq_lengths, log_total, grad_cols)
    )
    grad_queries = from_heads(grad_query_cols)
    grad_keys = from_heads(grad_key_cols)
    grad_values = from_heads(grad_value_cols)
    grads = (
        weight_grad(rows, grad_queries),
        column_sum(grad_queries),
        weight_grad(rows, grad_keys),
        weight_grad(rows, grad_values),
        column_sum(grad_values),
        output_weight_grad,
        output_bias_grad,
        gain_one_grad,
        shift_one_grad,
        up_weight_grad,
        up_bias_grad,
        down_weight_grad,
        down_bias_grad,
        gain_two_grad,
        shift_two_grad,
    )
    grad_rows = grad_first + project_back(grad_queries, w_query) + project_back(grad_keys, w_key)
    grad_rows = grad_rows + project_back(grad_values, w_value)
    return (grad_rows.astype(jnp.bfloat16), grads)


def local(
    tokens,
    cotangent,
    lengths,
    mb_count,
    query_weight,
    query_bias,
    key_weight,
    value_weight,
    value_bias,
    output_weight,
    output_bias,
    first_gain,
    first_shift,
    up_weight,
    up_bias,
    down_weight,
    down_bias,
    second_gain,
    second_shift,
):
    shards = (
        query_weight,
        query_bias,
        key_weight,
        value_weight,
        value_bias,
        output_weight,
        output_bias,
        first_gain,
        first_shift,
        up_weight,
        up_bias,
        down_weight,
        down_bias,
        second_gain,
        second_shift,
    )
    group_size = lax.axis_size("fsdp")
    slot_rows = tokens.shape[0] // MB_CAP
    slot_seqs = lengths.shape[0] // MB_CAP
    group_count = mb_count[lax.axis_index("dp")]
    totals = tuple(
        (jnp.zeros((group_size * item.shape[0],) + item.shape[1:], jnp.float32) for item in shards)
    )
    results = []
    input_grads = []
    for slot_index in range(MB_CAP):
        gathered = (
            lax.all_gather(shards[0], "fsdp", axis=0, tiled=True),
            lax.all_gather(shards[1], "fsdp", axis=0, tiled=True),
            lax.all_gather(shards[2], "fsdp", axis=0, tiled=True),
            lax.all_gather(shards[3], "fsdp", axis=0, tiled=True),
            lax.all_gather(shards[4], "fsdp", axis=0, tiled=True),
            lax.all_gather(shards[5], "fsdp", axis=0, tiled=True),
            lax.all_gather(shards[6], "fsdp", axis=0, tiled=True),
            lax.all_gather(shards[7], "fsdp", axis=0, tiled=True),
            lax.all_gather(shards[8], "fsdp", axis=0, tiled=True),
            lax.all_gather(shards[9], "fsdp", axis=0, tiled=True),
            lax.all_gather(shards[10], "fsdp", axis=0, tiled=True),
            lax.all_gather(shards[11], "fsdp", axis=0, tiled=True),
            lax.all_gather(shards[12], "fsdp", axis=0, tiled=True),
            lax.all_gather(shards[13], "fsdp", axis=0, tiled=True),
            lax.all_gather(shards[14], "fsdp", axis=0, tiled=True),
        )
        rows = tokens[slot_index * slot_rows : (slot_index + 1) * slot_rows]
        seq_lengths = lengths[slot_index * slot_seqs : (slot_index + 1) * slot_seqs]
        result, saved = slot_forward(rows, gathered, seq_lengths, HEADS)
        results.append(result.astype(jnp.bfloat16))
        grad_out = cotangent[slot_index * slot_rows : (slot_index + 1) * slot_rows].astype(
            jnp.float32
        )

        def run_backward(carried):
            grad_rows, grads = slot_backward(rows, grad_out, saved, gathered, seq_lengths, HEADS)
            return (grad_rows, tuple((total + piece for total, piece in zip(carried, grads))))

        def skip_backward(carried):
            return (jnp.zeros_like(rows), carried)

        grad_rows, totals = lax.cond(slot_index < group_count, run_backward, skip_backward, totals)
        input_grads.append(grad_rows)
    pieces = jax.tree.map(
        lambda part: part.astype(jnp.float32),
        lax.psum_scatter(for_sending(totals), "fsdp", scatter_dimension=0, tiled=True),
    )
    summed = jax.tree.map(
        lambda part: part.astype(jnp.float32), lax.psum(for_sending(pieces), "dp")
    )
    return (jnp.concatenate(results, axis=0), jnp.concatenate(input_grads, axis=0)) + tuple(summed)


def solution(mesh):
    return jax.shard_map(
        local,
        mesh=mesh,
        in_specs=(
            P(("dp", "fsdp"), None),
            P(("dp", "fsdp"), None),
            P(("dp", "fsdp")),
            P(),
            P("fsdp", None),
            P("fsdp"),
            P("fsdp", None),
            P("fsdp", None),
            P("fsdp"),
            P("fsdp", None),
            P("fsdp"),
            P("fsdp"),
            P("fsdp"),
            P("fsdp", None),
            P("fsdp"),
            P("fsdp", None),
            P("fsdp"),
            P("fsdp"),
            P("fsdp"),
        ),
        out_specs=(
            P(("dp", "fsdp"), None),
            P(("dp", "fsdp"), None),
            P("fsdp", None),
            P("fsdp"),
            P("fsdp", None),
            P("fsdp", None),
            P("fsdp"),
            P("fsdp", None),
            P("fsdp"),
            P("fsdp"),
            P("fsdp"),
            P("fsdp", None),
            P("fsdp"),
            P("fsdp", None),
            P("fsdp"),
            P("fsdp"),
            P("fsdp"),
        ),
        check_vma=False,
    )
```

profile of v0, /device:TPU:0, one launch (start us, length us, event | category | flops | bytes accessed | tf_op | source)
XLA Modules:
  0.0 763.2 jit_solution(17119618371949956671)
XLA Ops:
  21.6 31.4 %all-reduce.18 = (bf16[768]{0:T(1024)(128)(2,1)S(1)}, bf16[768]{0:T(1024)(128)(2,1)S(1)}, bf16[768]{0:T(1024)(128)(2,1)S(1)}, bf16[768]{0:T(1024)(128)(2,1)S(1)}...) all-reduce(bf16[768]{0:T(1024)(128)(2,1)S(1)} %dynamic-update-slice, ...), channel_id=1, replica_groups=mesh['dp'=4,'fsdp'=8] {'fsdp'}, use_global_device_ids=true, to_apply=%add | all-reduce | flops 5376 | bytes 21504
  55.7 12.7 %all-gather = bf16[8,1,384]{2,1,0:T(2,128)(2,1)S(1)} all-gather(bf16[1,1,384]{2,1,0:T(2,128)(2,1)S(1)} %reshape.281), channel_id=1, replica_groups=mesh['dp'=4,'fsdp'=8] {'fsdp'}, dimensions={0}, use_global_device_ids=true | all-gather | bytes 6912 | tf_op jit(solution)/shard_map/all_gather | solution.py:307
  96.5 11.1 %all-gather.14.cloned.1.call-done = bf16[768,768]{1,0:T(8,128)(2,1)} async-done(((bf16[96,768]{1,0:T(8,128)(2,1)}), bf16[768,768]{1,0:T(8,128)(2,1)}) %all-gather.14.cloned.1.call-update) | async-done | bytes 1179664 | tf_op jit(solution)/shard_map/all_gather | solution.py:302
  136.6 23.4 %all-gather.16.cloned.1.call-done = bf16[768,3072]{1,0:T(8,128)(2,1)} async-done(((bf16[96,3072]{1,0:T(8,128)(2,1)}), bf16[768,3072]{1,0:T(8,128)(2,1)}) %all-gather.16.cloned.1.call-update) | async-done | bytes 4718608 | tf_op jit(solution)/shard_map/all_gather | solution.py:306
  160.0 18.8 %fusion.76 = (bf16[512,3072]{1,0:T(8,128)(2,1)}, f32[512,3072]{1,0:T(8,128)}) fusion(f32[3072]{0:T(1024)S(1)} %bitcast.279, bf16[512,768]{1,0:T(8,128)(2,1)} %get-tuple-element.852, bf16[768,3072]{1,0:T(8,128)(2,1)} %all-gather.16.cloned.1.call-done), kind=kOutput, calls=%fused_computation.162 | convolution fusion | flops 2519728128 | bytes 14954496 | tf_op jit(solution)/shard_map/dot_general | solution.py:93
  178.7 32.7 %all-gather.18.cloned.1.call-done = bf16[3072,768]{1,0:T(8,128)(2,1)} async-done(((bf16[384,768]{1,0:T(8,128)(2,1)}), bf16[3072,768]{1,0:T(8,128)(2,1)}) %all-gather.18.cloned.1.call-update) | async-done | bytes 4718608 | tf_op jit(solution)/shard_map/all_gather | solution.py:308
  211.5 6.1 fusion.115
  218.3 18.2 %fusion.79 = (bf16[512,3072]{1,0:T(8,128)(2,1)S(1)}, f32[512,3072]{1,0:T(8,128)}) fusion(f32[3072]{0:T(1024)S(1)} %bitcast.280, bf16[512,768]{1,0:T(8,128)(2,1)S(1)} %copy-done.50, bf16[768,3072]{1,0:T(8,128)(2,1)S(1)} %copy-done.97), kind=kOutput, calls=%fused_computation.165 | convolution fusion | flops 2519728128 | bytes 14954496 | tf_op jit(solution)/shard_map/dot_general | solution.py:93
  241.4 90.8 %conditional.2 = (bf16[512,768]{1,0:T(8,128)(2,1)}, f32[768,768]{0,1:T(8,128)S(1)}, f32[768]{0:T(1024)S(1)}, f32[768,768]{0,1:T(8,128)}, f32[768,768]{0,1:T(8,12...) conditional(s32[]{:T(128)} %bitcast.104, () %tuple.36, ...), branch_computations={%region_12.13_spmd, %region_13.28_spmd} | conditional | flops 16691619840 | bytes 337698560 | solution.py:328
  241.6 6.4 fusion.22
  249.7 17.9 %convert_reduce_fusion = (f32[3072]{0:T(1024)S(1)}, bf16[512,3072]{1,0:T(8,128)(2,1)S(1)}) fusion(f32[512,3072]{1,0:T(8,128)S(1)} %get-tuple-element.439, bf16[3072,768]{1,0:T(8,128)(2,1)S(1)} %get-tuple-element.440, f32[512,768]{1,0:T(8,128)S(1)} %get-tuple-element.845), kind=kOutput, calls=%fused_computation.10 | convolution fusion | flops 2532701184 | bytes 15740928 | tf_op jit(solution)/shard_map/cond/branch_1_fun/rc,dc->rd/dot_general | solution.py:97
  275.2 11.7 %multiply_reduce_fusion = (f32[12,512]{1,0:T(8,128)S(1)}, f32[12,512,512]{1,2,0:T(8,128)}) fusion(f32[12,512,512]{1,2,0:T(8,128)} %fusion.22, f32[12,512]{1,0:T(8,128)S(1)} %log_add_fusion, pred[512]{0:T(512)(128)(4,1)S(1)} %iota_compare_fusion, bf16[12,64,512]{2,1,0:T(8,128)(2,1)} %bitcast.259, bf16[1,12,64,512]{3,2,1,0:T(8,128)(2,1)S(1)} %copy-done.41), kind=kOutput, calls=%fused_computation.1 | convolution fusion | flops 418375680 | bytes 26788352 | tf_op jit(solution)/shard_map/cond/branch_1_fun/while/body/eval_jaxpr/hdq,hdk->hqk/dot_general | solution.py:73
  288.0 7.4 multiply_convert_fusion
  318.5 8.4 %convolution_bitcast_fusion.1 = f32[768,3072]{0,1:T(8,128)} fusion(bf16[512,3072]{1,0:T(8,128)(2,1)} %copy-done.106, bf16[512,768]{1,0:T(8,128)(2,1)} %get-tuple-element.456), kind=kOutput, calls=%fused_computation.29 | convolution fusion | flops 2415919104 | bytes 13369344 | tf_op jit(solution)/shard_map/cond/branch_1_fun/rc,rd->cd/dot_general | solution.py:101
  332.8 99.3 %conditional.3 = (bf16[512,768]{1,0:T(8,128)(2,1)}, f32[768,768]{0,1:T(8,128)S(1)}, f32[768]{0:T(1024)S(1)}, f32[768,768]{0,1:T(8,128)}, f32[768,768]{0,1:T(8,12...) conditional(s32[]{:T(128)} %bitcast.110, ...), branch_computations={%region_28.29_spmd, %region_29.44_spmd} | conditional | flops 16698708992 | bytes 455893312 | solution.py:328
  332.9 7.7 %fusion.57 = f32[12,512,512]{1,2,0:T(8,128)} fusion(bf16[1,12,64,512]{3,2,1,0:T(8,128)(2,1)S(1)} %get-tuple-element.487, bf16[1,12,64,512]{3,2,1,0:T(8,128)(2,1)} %get-tuple-element.486), kind=kOutput, calls=%fused_computation.129 | convolution fusion | flops 402653184 | bytes 14155776 | tf_op jit(solution)/shard_map/cond/branch_1_fun/while/body/eval_jaxpr/hdq,hdk->hqk/dot_general | solution.py:51
  343.5 17.8 %convert_reduce_fusion.5 = (f32[3072]{0:T(1024)S(1)}, bf16[512,3072]{1,0:T(8,128)(2,1)S(1)}) fusion(f32[512,3072]{1,0:T(8,128)S(1)} %copy-done.107, bf16[3072,768]{1,0:T(8,128)(2,1)S(1)} %bitcast.290, f32[512,768]{1,0:T(8,128)S(1)} %get-tuple-element.849), kind=kOutput, calls=%fused_computation.86 | convolution fusion | flops 2532701184 | bytes 15740928 | tf_op jit(solution)/shard_map/cond/branch_1_fun/rc,dc->rd/dot_general | solution.py:97
  369.9 11.8 %multiply_reduce_fusion.7 = (f32[12,512]{1,0:T(8,128)S(1)}, f32[12,512,512]{1,2,0:T(8,128)}) fusion(f32[12,512,512]{1,2,0:T(8,128)} %fusion.57, f32[12,512]{1,0:T(8,128)S(1)} %log_add_fusion.1, pred[512]{0:T(512)(128)(4,1)S(1)} %iota_compare_fusion.1, bf16[12,64,512]{2,1,0:T(8,128)(2,1)} %bitcast.261, bf16[1,12,64,512]{3,2,1,0:T(8,128)(2,1)} %get-tuple-element.491), kind=kOutput, calls=%fused_computation.75 | convolution fusion | flops 418375680 | bytes 26788352 | tf_op jit(solution)/shard_map/cond/branch_1_fun/while/body/eval_jaxpr/hdq,hdk->hqk/dot_general | solution.py:73
  383.0 7.6 %multiply_convert_fusion.3 = bf16[12,512,512]{1,2,0:T(8,128)(2,1)S(1)} fusion(f32[12,512,512]{1,2,0:T(8,128)} %get-tuple-element.873, f32[12,512,512]{1,2,0:T(8,128)S(1)} %bitcast.242, f32[12,512]{1,0:T(8,128)S(1)} %get-tuple-element.872, f32[12,512]{1,0:T(8,128)S(1)} %log_add_fusion.1, pred[512]{0:T(512)(128)(4,1)S(1)} %iota_compare_fusion.1), kind=kLoop, calls=%fused_computation.74 | loop fusion | flops 18874368 | bytes 31506944 | tf_op jit(solution)/shard_map/cond/branch_1_fun/while/body/eval_jaxpr/convert_element_type | solution.py:80
  415.7 7.5 bitcast_add_fusion.1
  423.3 7.4 bitcast_add_fusion
  442.0 7.7 %copy.106 = bf16[768,3072]{1,0:T(8,128)(2,1)} copy(f32[768,3072]{0,1:T(8,128)} %get-tuple-element.589) | data formatting | bytes 14155776 | tf_op jit(solution)/shard_map/cond | solution.py:328
  449.8 7.7 %copy.107 = bf16[3072,768]{1,0:T(8,128)(2,1)} copy(f32[3072,768]{0,1:T(8,128)} %get-tuple-element.591) | data formatting | bytes 14155776 | tf_op jit(solution)/shard_map/cond | solution.py:328
  457.6 7.9 %reduce-scatter.7.cloned.1.call-done = bf16[96,768]{1,0:T(8,128)(2,1)} async-done(((bf16[768,768]{1,0:T(8,128)(2,1)}), bf16[96,768]{1,0:T(8,128)(2,1)}) %reduce-scatter.7.cloned.1.call-update) | async-done | bytes 147472 | tf_op jit(solution)/shard_map/reduce_scatter | solution.py:332
  465.5 34.0 %reduce-scatter.9.cloned.1.call-done = bf16[96,768]{1,0:T(8,128)(2,1)} async-done(((bf16[768,768]{1,0:T(8,128)(2,1)}), bf16[96,768]{1,0:T(8,128)(2,1)}) %reduce-scatter.9.cloned.1.call-update) | async-done | bytes 147472 | tf_op jit(solution)/shard_map/reduce_scatter | solution.py:332
  499.5 34.0 %reduce-scatter.11.cloned.1.call-done = bf16[96,768]{1,0:T(8,128)(2,1)} async-done(((bf16[768,768]{1,0:T(8,128)(2,1)}), bf16[96,768]{1,0:T(8,128)(2,1)}) %reduce-scatter.11.cloned.1.call-update) | async-done | bytes 147472 | tf_op jit(solution)/shard_map/reduce_scatter | solution.py:332
  533.6 33.9 %reduce-scatter.13.cloned.1.call-done = bf16[96,768]{1,0:T(8,128)(2,1)} async-done(((bf16[768,768]{1,0:T(8,128)(2,1)}), bf16[96,768]{1,0:T(8,128)(2,1)}) %reduce-scatter.13.cloned.1.call-update) | async-done | bytes 147472 | tf_op jit(solution)/shard_map/reduce_scatter | solution.py:332
  567.5 55.4 %reduce-scatter.15.cloned.1.call-done = bf16[96,3072]{1,0:T(8,128)(2,1)} async-done(((bf16[768,3072]{1,0:T(8,128)(2,1)}), bf16[96,3072]{1,0:T(8,128)(2,1)}) %reduce-scatter.15.cloned.1.call-update) | async-done | bytes 589840 | tf_op jit(solution)/shard_map/reduce_scatter | solution.py:332
  622.8 55.5 %reduce-scatter.17.cloned.1.call-done = bf16[384,768]{1,0:T(8,128)(2,1)} async-done(((bf16[3072,768]{1,0:T(8,128)(2,1)}), bf16[384,768]{1,0:T(8,128)(2,1)}) %reduce-scatter.17.cloned.1.call-update) | async-done | bytes 589840 | tf_op jit(solution)/shard_map/reduce_scatter | solution.py:332
  680.1 26.0 %all-reduce.17 = (bf16[768]{0:T(1024)(128)(2,1)S(1)}, bf16[768]{0:T(1024)(128)(2,1)S(1)}, bf16[768]{0:T(1024)(128)(2,1)S(1)}, bf16[768]{0:T(1024)(128)(2,1)S(1)}...) all-reduce(bf16[768]{0:T(1024)(128)(2,1)S(1)} %dynamic-update-slice, ...), channel_id=1, replica_groups=mesh['dp'=4,'fsdp'=8] {'fsdp'}, use_global_device_ids=true, to_apply=%add.7 | all-reduce | flops 9984 | bytes 39936
  706.8 10.0 %all-reduce.19 = (bf16[96]{0:T(256)(128)(2,1)S(1)}, bf16[96]{0:T(256)(128)(2,1)S(1)}, bf16[96]{0:T(256)(128)(2,1)S(1)}, bf16[96]{0:T(256)(128)(2,1)S(1)}, bf16[9...) all-reduce(bf16[96]{0:T(256)(128)(2,1)S(1)} %dynamic-slice.17, ...), channel_id=1, replica_groups=mesh['dp'=4,'fsdp'=8] {'dp'}, use_global_device_ids=true, to_apply=%region_47.48 | all-reduce | flops 1152 | bytes 4608 | tf_op jit(solution)/shard_map/psum | solution.py:335
  725.9 19.7 %all-reduce.23.cloned.1.call-done = (bf16[96,768]{1,0:T(8,128)(2,1)}, bf16[96,768]{1,0:T(8,128)(2,1)}, bf16[96,768]{1,0:T(8,128)(2,1)}, bf16[96,768]{1,0:T(8,128...) async-done(((bf16[96,768]{1,0:T(8,128)(2,1)}, bf16[96,768]{1,0:T(8,128)(2,1)}, bf16[96,768]{1,0:T(8,128)(2,1)}, bf16[96,768]{1,0:T(8,128)(2,1)}, ...) | async-done | bytes 1769488 | tf_op jit(solution)/shard_map/psum | solution.py:335
  (450 shorter events, 185.4 us)
Async XLA Ops:
  7.2 66.0 %copy-start.54 = (bf16[1024,768]{1,0:T(8,128)(2,1)S(1)}, bf16[1024,768]{1,0:T(8,128)(2,1)}, u32[]{:S(2)}) copy-start(bf16[1024,768]{1,0:T(8,128)(2,1)} %param.23) | copy-start | bytes 4718596
  7.2 66.0 %all-gather.8.cloned.1.call-start = ((), (), s32[]{:S(2)}) async-start(), calls=%async_computation.6 | async-start | bytes 1327104 | tf_op jit(solution)/shard_map/all_gather | solution.py:300
  7.9 67.7 %all-gather.10.cloned.1.call-start = ((), (), s32[]{:S(2)}) async-start(), calls=%async_computation.7 | async-start | bytes 1327104 | tf_op jit(solution)/shard_map/all_gather | solution.py:297
  8.7 75.0 %all-gather.12.cloned.1.call-start = ((), (), s32[]{:S(2)}) async-start(), calls=%async_computation.8 | async-start | bytes 1327104 | tf_op jit(solution)/shard_map/all_gather | solution.py:299
  9.4 98.2 %all-gather.14.cloned.1.call-start = ((), (), s32[]{:S(2)}) async-start(), calls=%async_computation.9 | async-start | bytes 1327104 | tf_op jit(solution)/shard_map/all_gather | solution.py:302
  10.0 150.0 %all-gather.16.cloned.1.call-start = ((), (), s32[]{:S(2)}) async-start(), calls=%async_computation.10 | async-start | bytes 5308416 | tf_op jit(solution)/shard_map/all_gather | solution.py:306
  10.6 200.9 %all-gather.18.cloned.1.call-start = ((), (), s32[]{:S(2)}) async-start(), calls=%async_computation.11 | async-start | bytes 5308416 | tf_op jit(solution)/shard_map/all_gather | solution.py:308
  11.2 454.4 %reduce-scatter.7.cloned.1.call-start = ((), (), s32[]{:S(2)}) async-start(), calls=%async_computation.12 | async-start | bytes 1327104 | tf_op jit(solution)/shard_map/reduce_scatter | solution.py:332
  136.5 74.9 %copy-start.32 = (f32[512,768]{1,0:T(8,128)}, f32[512,768]{1,0:T(8,128)S(1)}, u32[]{:S(2)}) copy-start(f32[512,768]{1,0:T(8,128)S(1)} %get-tuple-element.853) | copy-start | bytes 4718596
  136.5 99.9 %copy-start.30 = (f32[512,768]{1,0:T(8,128)}, f32[512,768]{1,0:T(8,128)S(1)}, u32[]{:S(2)}) copy-start(f32[512,768]{1,0:T(8,128)S(1)} %get-tuple-element.889) | copy-start | bytes 4718596
  218.0 23.2 %slice-start.12 = ((s8[6291456]{0:T(1024)(128)(4,1)}), s8[4194304]{0:T(1024)(128)(4,1)S(1)}, s32[]{:S(2)}) async-start(s8[6291456]{0:T(1024)(128)(4,1)} %bitcast.291), calls=%async_computation.31 | async-start | bytes 8388608
  241.3 91.5 %copy-start.1 = (bf16[512,768]{0,1:T(8,128)(2,1)S(1)}, bf16[512,768]{0,1:T(8,128)(2,1)}, u32[]{:S(2)}) copy-start(bf16[512,768]{0,1:T(8,128)(2,1)} %copy-done) | copy-start | bytes 2359300
  241.3 91.5 %copy-start.60 = (f32[12,512]{1,0:T(8,128)S(1)}, f32[12,512]{1,0:T(8,128)}, u32[]{:S(2)}) copy-start(f32[12,512]{1,0:T(8,128)} %copy-done.59) | copy-start | bytes 73732
  241.3 91.4 %copy-start.64 = (f32[12,512]{1,0:T(8,128)S(1)}, f32[12,512]{1,0:T(8,128)}, u32[]{:S(2)}) copy-start(f32[12,512]{1,0:T(8,128)} %copy-done.63) | copy-start | bytes 73732
  241.3 91.4 %copy-start.90 = (f32[512]{0:T(512)S(1)}, f32[512]{0:T(512)}, u32[]{:S(2)}) copy-start(f32[512]{0:T(512)} %copy-done.89) | copy-start | bytes 6148
  271.1 33.7 %copy-start.9 = (f32[512,768]{1,0:T(8,128)}, f32[512,768]{1,0:T(8,128)S(1)}, u32[]{:S(2)}) copy-start(f32[512,768]{1,0:T(8,128)S(1)} %get-tuple-element.847) | copy-start | bytes 4718596 | tf_op jit(solution)/shard_map/cond
  433.6 65.9 %reduce-scatter.9.cloned.1.call-start = ((), (), s32[]{:S(2)}) async-start(), calls=%async_computation.13 | async-start | bytes 1327104 | tf_op jit(solution)/shard_map/reduce_scatter | solution.py:332
  436.4 97.1 %reduce-scatter.11.cloned.1.call-start = ((), (), s32[]{:S(2)}) async-start(), calls=%async_computation.14 | async-start | bytes 1327104 | tf_op jit(solution)/shard_map/reduce_scatter | solution.py:332
  439.2 128.3 %reduce-scatter.13.cloned.1.call-start = ((), (), s32[]{:S(2)}) async-start(), calls=%async_computation.15 | async-start | bytes 1327104 | tf_op jit(solution)/shard_map/reduce_scatter | solution.py:332
  441.9 180.9 %reduce-scatter.15.cloned.1.call-start = ((), (), s32[]{:S(2)}) async-start(), calls=%async_computation.16 | async-start | bytes 5308416 | tf_op jit(solution)/shard_map/reduce_scatter | solution.py:332
  449.7 228.7 %reduce-scatter.17.cloned.1.call-start = ((), (), s32[]{:S(2)}) async-start(), calls=%async_computation.17 | async-start | bytes 5308416 | tf_op jit(solution)/shard_map/reduce_scatter | solution.py:332
  457.5 222.3 %copy-start.105 = (bf16[96]{0:T(256)(128)(2,1)S(1)}, bf16[96]{0:T(256)(128)(2,1)}, u32[]{:S(2)}) copy-start(bf16[96]{0:T(256)(128)(2,1)} %param.41) | copy-start | bytes 580
  457.5 222.6 %copy-start.70 = (f32[768]{0:T(1024)S(1)}, f32[768]{0:T(1024)}, u32[]{:S(2)}) copy-start(f32[768]{0:T(1024)} %get-tuple-element.592) | copy-start | bytes 9220
  457.5 222.6 %copy-start.74 = (f32[768]{0:T(1024)S(1)}, f32[768]{0:T(1024)}, u32[]{:S(2)}) copy-start(f32[768]{0:T(1024)} %get-tuple-element.593) | copy-start | bytes 9220
  457.5 222.6 %copy-start.78 = (f32[768]{0:T(1024)S(1)}, f32[768]{0:T(1024)}, u32[]{:S(2)}) copy-start(f32[768]{0:T(1024)} %get-tuple-element.594) | copy-start | bytes 9220
  457.5 264.0 %copy-start.11 = (f32[512,768]{1,0:T(8,128)S(1)}, f32[512,768]{1,0:T(8,128)}, u32[]{:S(2)}) copy-start(f32[512,768]{1,0:T(8,128)} %copy-done.10) | copy-start | bytes 4718596
  457.5 264.0 %copy-start.13 = (f32[512,768]{1,0:T(8,128)S(1)}, f32[512,768]{1,0:T(8,128)}, u32[]{:S(2)}) copy-start(f32[512,768]{1,0:T(8,128)} %copy-done.12) | copy-start | bytes 4718596
  457.5 264.0 %copy-start.80 = (f32[512]{0:T(512)S(1)}, f32[512]{0:T(512)}, u32[]{:S(2)}) copy-start(f32[512]{0:T(512)} %copy-done.79) | copy-start | bytes 6148
  457.5 264.0 %copy-start.82 = (f32[512]{0:T(512)S(1)}, f32[512]{0:T(512)}, u32[]{:S(2)}) copy-start(f32[512]{0:T(512)} %copy-done.81) | copy-start | bytes 6148
  457.5 264.0 %copy-start.84 = (f32[512]{0:T(512)S(1)}, f32[512]{0:T(512)}, u32[]{:S(2)}) copy-start(f32[512]{0:T(512)} %copy-done.83) | copy-start | bytes 6148
  457.5 264.0 %copy-start.86 = (f32[512]{0:T(512)S(1)}, f32[512]{0:T(512)}, u32[]{:S(2)}) copy-start(f32[512]{0:T(512)} %copy-done.85) | copy-start | bytes 6148
  457.6 288.0 %all-reduce.23.cloned.1.call-start = ((), (), s32[]{:S(2)}) async-start(), calls=%async_computation.18 | async-start | bytes 3538944 | tf_op jit(solution)/shard_map/psum | solution.py:335
  (103 other events, 701.4 us)
Sparse Core Ops, SparseCore 0:
  9.6 25.8 all-gather.7
  37.2 22.3 all-gather.9
  61.2 22.3 all-gather.11
  85.1 22.4 all-gather.13
  109.1 50.8 all-gather.15
  161.5 49.9 all-gather.17
  433.8 31.6 reduce-scatter.6
  468.4 31.1 reduce-scatter.8
  502.4 31.1 reduce-scatter.10
  536.3 31.1 reduce-scatter.12
  569.8 53.0 reduce-scatter.14
  625.0 53.3 reduce-scatter.16
  682.2 63.3 all-reduce.22
where the time goes:
time: 775 us; the launch traced here: 763 us
  waiting for transfers between devices  317 us (41%)
  matrix products  238 us (31%)
  blocking collectives  80.1 us (10%)
  other arithmetic  55.6 us (7%)
  local copies, waits for them, and re-layouts  52.5 us (7%)
  between operations  18.5 us (2%)
    reduce_scatter x6, waiting for transfers between devices, local(): lax.psum_scatter(for_sending(totals), 'fsdp', scatter_dimension=0, tiled=...  221 us
    dot_general x12, matrix products, project(): return jnp.dot(left, right, preferred_element_type=jnp.float32)  65.3 us
    unnamed x2, blocking collectives  57.4 us
    dot_general x12, matrix products, project_back(): jnp.einsum('rc,dc->rd', left, right, preferred_element_type=jnp.float32)  54.2 us
    dot_general x12, matrix products, weight_grad(): jnp.einsum('rc,rd->cd', left, right, preferred_element_type=jnp.float32)  53.8 us
    all_gather x1, waiting for transfers between devices, local(): lax.all_gather(shards[11], 'fsdp', axis=0, tiled=True)  32.7 us
    cond x6, local copies, waits for them, and re-layouts, local(): lax.cond(slot_index < group_count, run_backward, skip_backward, totals)  24.9 us
    dot_general x2, matrix products, attend_backward(): jnp.einsum('hdq,hdk->hqk', grad_cols, value_cols, preferred_element_type=...  23.5 us
  transfers between devices with their start and end apart: 13, of which 11 were waited for; matrix products, arithmetic and copies ran while one was open for 15% of the time, Pallas kernels for 0%

commit v1 on v0

--- a/solution.py
+++ b/solution.py
@@ -6,6 +6,37 @@
 HEADS = 12
 MB_CAP = 2
 norm_epsilon = 1e-05
+
+
+def _order_sample(here_x, dim_no):
+    last = list(here_x.shape[1:])
+    last[dim_no] *= here_x.shape[0]
+    res = jnp.moveaxis(here_x, 0, dim_no).reshape(last)
+    return res
+
+
+def divide_tasks(a0, along_axis):
+    extra = jax.lax.axis_size(along_axis)
+    before = jax.lax.axis_index(along_axis)
+    finding, s_next = (extra, before)
+    t_next, arr_next = (a0[None], 1)
+    while arr_next < finding:
+        series = []
+        for dev_i in range(finding):
+            series.append((dev_i, dev_i ^ arr_next))
+        formed = jax.lax.ppermute(t_next, along_axis, series)
+        long_array = s_next & arr_next == 0
+        view_out = jnp.where(long_array, t_next, formed)
+        answer = jnp.where(long_array, formed, t_next)
+        t_next = jnp.concatenate([view_out, answer])
+        arr_next *= 2
+    return t_next
+
+
+def guide_sectors(frame, vector, d_out):
+    tall = divide_tasks(frame, vector)
+    field_out = _order_sample(tall, d_out)
+    return field_out
 
 
 def for_sending(shard):
@@ -303,7 +334,7 @@
             lax.all_gather(shards[6], "fsdp", axis=0, tiled=True),
             lax.all_gather(shards[7], "fsdp", axis=0, tiled=True),
             lax.all_gather(shards[8], "fsdp", axis=0, tiled=True),
-            lax.all_gather(shards[9], "fsdp", axis=0, tiled=True),
+            guide_sectors(shards[9], "fsdp", 0),
             lax.all_gather(shards[10], "fsdp", axis=0, tiled=True),
             lax.all_gather(shards[11], "fsdp", axis=0, tiled=True),
             lax.all_gather(shards[12], "fsdp", axis=0, tiled=True),

time: 775 us -> 833 us (1.075)
  waiting for transfers between devices: 317 us -> 346 us
  blocking collectives: 80.1 us -> 98.5 us
  other arithmetic: 55.6 us -> 65.6 us
    ppermute x0 -> x3, waiting for transfers between devices: none -> 80.1 us  [divide_tasks(): formed = jax.lax.ppermute(t_next, along_axis, series)]
    all_gather x1, waiting for transfers between devices: 32.7 us -> 0.01 us  [local(): lax.all_gather(shards[11], 'fsdp', axis=0, tiled=True)]
    all_gather x1 -> x0, waiting for transfers between devices: 23.4 us -> none  [local(): lax.all_gather(shards[9], 'fsdp', axis=0, tiled=True)]
    unnamed x2, blocking collectives: 57.4 us -> 75.2 us
    all_gather x1, waiting for transfers between devices: 11.1 us -> 22.7 us  [local(): lax.all_gather(shards[5], 'fsdp', axis=0, tiled=True)]
  transfers between devices with their start and end apart: 13 -> 15, of which waited for: 11 -> 10; matrix products, arithmetic and copies ran while one was open for 15% -> 17% of each run, Pallas kernels for 0% -> 0%
where the time goes in v1:
time: 833 us; the launch traced here: 829 us
  waiting for transfers between devices  346 us (42%)
  matrix products  237 us (28%)
  blocking collectives  98.5 us (12%)
  other arithmetic  65.6 us (8%)
  local copies, waits for them, and re-layouts  56.9 us (7%)
  between operations  18.7 us (2%)
    reduce_scatter x6, waiting for transfers between devices, local(): lax.psum_scatter(for_sending(totals), 'fsdp', scatter_dimension=0, tiled=...  221 us
    ppermute x3, waiting for transfers between devices, divide_tasks(): formed = jax.lax.ppermute(t_next, along_axis, series)  80.1 us
    unnamed x2, blocking collectives  75.2 us
    dot_general x12, matrix products, project(): return jnp.dot(left, right, preferred_element_type=jnp.float32)  64.1 us
    dot_general x12, matrix products, weight_grad(): jnp.einsum('rc,rd->cd', left, right, preferred_element_type=jnp.float32)  53.9 us
    dot_general x12, matrix products, project_back(): jnp.einsum('rc,dc->rd', left, right, preferred_element_type=jnp.float32)  53.8 us
    cond x6, local copies, waits for them, and re-layouts, local(): lax.cond(slot_index < group_count, run_backward, skip_backward, totals)  25 us
    dot_general x2, matrix products, attend_backward(): jnp.einsum('hdq,hdk->hqk', grad_cols, value_cols, preferred_element_type=...  23.5 us
  transfers between devices with their start and end apart: 15, of which 10 were waited for; matrix products, arithmetic and copies ran while one was open for 17% of the time, Pallas kernels for 0%

profile of v1, /device:TPU:0, one launch (start us, length us, event | category | flops | bytes accessed | tf_op | source)
XLA Modules:
  0.0 829.3 jit_solution(17195513216065395185)
XLA Ops:
  27.5 49.1 %all-reduce.18 = (bf16[768]{0:T(1024)(128)(2,1)S(1)}, bf16[768]{0:T(1024)(128)(2,1)S(1)}, bf16[768]{0:T(1024)(128)(2,1)S(1)}, bf16[768]{0:T(1024)(128)(2,1)S(1)}...) all-reduce(bf16[768]{0:T(1024)(128)(2,1)S(1)} %dynamic-update-slice, ...), channel_id=1, replica_groups=mesh['dp'=4,'fsdp'=8] {'fsdp'}, use_global_device_ids=true, to_apply=%add | all-reduce | flops 5376 | bytes 21504
  78.6 13.4 %all-gather = bf16[8,1,384]{2,1,0:T(2,128)(2,1)S(1)} all-gather(bf16[1,1,384]{2,1,0:T(2,128)(2,1)S(1)} %reshape.286), channel_id=1, replica_groups=mesh['dp'=4,'fsdp'=8] {'fsdp'}, dimensions={0}, use_global_device_ids=true | all-gather | bytes 6912 | tf_op jit(solution)/shard_map/all_gather | solution.py:338
  146.2 22.7 %all-gather.13.cloned.1.call-done = bf16[768,768]{1,0:T(8,128)(2,1)} async-done(((bf16[96,768]{1,0:T(8,128)(2,1)}), bf16[768,768]{1,0:T(8,128)(2,1)}) %all-gather.13.cloned.1.call-update) | async-done | bytes 1179664 | tf_op jit(solution)/shard_map/all_gather | solution.py:333
  174.8 78.3 %collective-permute-done.2 = bf16[4,96,3072]{2,1,0:T(8,128)(2,1)} collective-permute-done((bf16[4,96,3072]{2,1,0:T(8,128)(2,1)}, bf16[4,96,3072]{2,1,0:T(8,128)(2,1)}, u32[]{:S(2)}, u32[]{:S(2)}) %collective-permute-start.2) | collective-permute-done | bytes 2359328 | tf_op jit(solution)/shard_map/ppermute | solution.py:27
  255.7 18.7 %fusion.76 = (bf16[512,3072]{1,0:T(8,128)(2,1)}, f32[512,3072]{1,0:T(8,128)}) fusion(f32[3072]{0:T(1024)S(1)} %bitcast.292, bf16[512,768]{1,0:T(8,128)(2,1)S(1)} %get-tuple-element.852, bf16[768,3072]{1,0:T(8,128)(2,1)S(1)} %bitcast.259), kind=kOutput, calls=%fused_computation.162 | convolution fusion | flops 2519728128 | bytes 14954496 | tf_op jit(solution)/shard_map/dot_general | solution.py:124
  274.5 18.4 %fusion.79 = (bf16[512,3072]{1,0:T(8,128)(2,1)}, f32[512,3072]{1,0:T(8,128)}) fusion(f32[3072]{0:T(1024)S(1)} %bitcast.293, bf16[512,768]{1,0:T(8,128)(2,1)S(1)} %get-tuple-element.894, bf16[768,3072]{1,0:T(8,128)(2,1)S(1)} %bitcast.260), kind=kOutput, calls=%fused_computation.165 | convolution fusion | flops 2519728128 | bytes 14954496 | tf_op jit(solution)/shard_map/dot_general | solution.py:124
  292.9 6.1 fusion.115
  306.9 90.7 %conditional.2 = (bf16[512,768]{1,0:T(8,128)(2,1)}, f32[768,768]{0,1:T(8,128)S(1)}, f32[768]{0:T(1024)S(1)}, f32[768,768]{0,1:T(8,128)}, f32[768,768]{0,1:T(8,12...) conditional(s32[]{:T(128)} %bitcast.106, () %tuple.36, ...), branch_computations={%region_12.13_spmd, %region_13.28_spmd} | conditional | flops 16691619840 | bytes 337698560 | solution.py:359
  307.1 6.4 fusion.22
  315.2 17.5 %convert_reduce_fusion = (f32[3072]{0:T(1024)S(1)}, bf16[512,3072]{1,0:T(8,128)(2,1)S(1)}) fusion(f32[512,3072]{1,0:T(8,128)S(1)} %get-tuple-element.439, bf16[3072,768]{1,0:T(8,128)(2,1)S(1)} %get-tuple-element.440, f32[512,768]{1,0:T(8,128)S(1)} %get-tuple-element.845), kind=kOutput, calls=%fused_computation.10 | convolution fusion | flops 2532701184 | bytes 15740928 | tf_op jit(solution)/shard_map/cond/branch_1_fun/rc,dc->rd/dot_general | solution.py:128
  340.3 11.7 %multiply_reduce_fusion = (f32[12,512]{1,0:T(8,128)S(1)}, f32[12,512,512]{1,2,0:T(8,128)}) fusion(f32[12,512,512]{1,2,0:T(8,128)} %fusion.22, f32[12,512]{1,0:T(8,128)S(1)} %log_add_fusion, pred[512]{0:T(512)(128)(4,1)S(1)} %iota_compare_fusion, bf16[12,64,512]{2,1,0:T(8,128)(2,1)} %bitcast.271, bf16[1,12,64,512]{3,2,1,0:T(8,128)(2,1)S(1)} %copy-done.40), kind=kOutput, calls=%fused_computation.1 | convolution fusion | flops 418375680 | bytes 26788352 | tf_op jit(solution)/shard_map/cond/branch_1_fun/while/body/eval_jaxpr/hdq,hdk->hqk/dot_general | solution.py:104
  353.1 7.4 multiply_convert_fusion
  383.7 8.4 %convolution_bitcast_fusion.1 = f32[768,3072]{0,1:T(8,128)} fusion(bf16[512,3072]{1,0:T(8,128)(2,1)} %copy-done.111, bf16[512,768]{1,0:T(8,128)(2,1)} %get-tuple-element.456), kind=kOutput, calls=%fused_computation.29 | convolution fusion | flops 2415919104 | bytes 13369344 | tf_op jit(solution)/shard_map/cond/branch_1_fun/rc,rd->cd/dot_general | solution.py:132
  392.1 5.0 convolution_bitcast_fusion
  398.2 99.2 %conditional.3 = (bf16[512,768]{1,0:T(8,128)(2,1)}, f32[768,768]{0,1:T(8,128)S(1)}, f32[768]{0:T(1024)S(1)}, f32[768,768]{0,1:T(8,128)}, f32[768,768]{0,1:T(8,12...) conditional(s32[]{:T(128)} %bitcast.112, ...), branch_computations={%region_28.29_spmd, %region_29.44_spmd} | conditional | flops 16698708992 | bytes 455893312 | solution.py:359
  398.2 7.7 fusion.57
  408.9 17.7 %convert_reduce_fusion.5 = (f32[3072]{0:T(1024)S(1)}, bf16[512,3072]{1,0:T(8,128)(2,1)S(1)}) fusion(f32[512,3072]{1,0:T(8,128)S(1)} %copy-done.112, bf16[3072,768]{1,0:T(8,128)(2,1)S(1)} %bitcast.299, f32[512,768]{1,0:T(8,128)S(1)} %get-tuple-element.849), kind=kOutput, calls=%fused_computation.86 | convolution fusion | flops 2532701184 | bytes 15740928 | tf_op jit(solution)/shard_map/cond/branch_1_fun/rc,dc->rd/dot_general | solution.py:128
  435.3 11.8 %multiply_reduce_fusion.7 = (f32[12,512]{1,0:T(8,128)S(1)}, f32[12,512,512]{1,2,0:T(8,128)}) fusion(f32[12,512,512]{1,2,0:T(8,128)} %fusion.57, f32[12,512]{1,0:T(8,128)S(1)} %log_add_fusion.1, pred[512]{0:T(512)(128)(4,1)S(1)} %iota_compare_fusion.1, bf16[12,64,512]{2,1,0:T(8,128)(2,1)} %bitcast.273, bf16[1,12,64,512]{3,2,1,0:T(8,128)(2,1)} %get-tuple-element.491), kind=kOutput, calls=%fused_computation.75 | convolution fusion | flops 418375680 | bytes 26788352 | tf_op jit(solution)/shard_map/cond/branch_1_fun/while/body/eval_jaxpr/hdq,hdk->hqk/dot_general | solution.py:104
  448.3 7.4 multiply_convert_fusion.3
  480.9 7.5 bitcast_add_fusion.1
  488.5 7.4 bitcast_add_fusion
  507.2 7.7 copy.106
  515.0 7.7 copy.107
  522.8 7.9 reduce-scatter.7.cloned.1.call-done
  530.8 34.3 %reduce-scatter.9.cloned.1.call-done = bf16[96,768]{1,0:T(8,128)(2,1)} async-done(((bf16[768,768]{1,0:T(8,128)(2,1)}), bf16[96,768]{1,0:T(8,128)(2,1)}) %reduce-scatter.9.cloned.1.call-update) | async-done | bytes 147472 | tf_op jit(solution)/shard_map/reduce_scatter | solution.py:363
  565.1 34.1 %reduce-scatter.11.cloned.1.call-done = bf16[96,768]{1,0:T(8,128)(2,1)} async-done(((bf16[768,768]{1,0:T(8,128)(2,1)}), bf16[96,768]{1,0:T(8,128)(2,1)}) %reduce-scatter.11.cloned.1.call-update) | async-done | bytes 147472 | tf_op jit(solution)/shard_map/reduce_scatter | solution.py:363
  599.1 34.2 %reduce-scatter.13.cloned.1.call-done = bf16[96,768]{1,0:T(8,128)(2,1)} async-done(((bf16[768,768]{1,0:T(8,128)(2,1)}), bf16[96,768]{1,0:T(8,128)(2,1)}) %reduce-scatter.13.cloned.1.call-update) | async-done | bytes 147472 | tf_op jit(solution)/shard_map/reduce_scatter | solution.py:363
  633.3 55.3 %reduce-scatter.15.cloned.1.call-done = bf16[96,3072]{1,0:T(8,128)(2,1)} async-done(((bf16[768,3072]{1,0:T(8,128)(2,1)}), bf16[96,3072]{1,0:T(8,128)(2,1)}) %reduce-scatter.15.cloned.1.call-update) | async-done | bytes 589840 | tf_op jit(solution)/shard_map/reduce_scatter | solution.py:363
  688.6 55.7 %reduce-scatter.17.cloned.1.call-done = bf16[384,768]{1,0:T(8,128)(2,1)} async-done(((bf16[3072,768]{1,0:T(8,128)(2,1)}), bf16[384,768]{1,0:T(8,128)(2,1)}) %reduce-scatter.17.cloned.1.call-update) | async-done | bytes 589840 | tf_op jit(solution)/shard_map/reduce_scatter | solution.py:363
  746.0 26.0 %all-reduce.17 = (bf16[768]{0:T(1024)(128)(2,1)S(1)}, bf16[768]{0:T(1024)(128)(2,1)S(1)}, bf16[768]{0:T(1024)(128)(2,1)S(1)}, bf16[768]{0:T(1024)(128)(2,1)S(1)}...) all-reduce(bf16[768]{0:T(1024)(128)(2,1)S(1)} %dynamic-update-slice, ...), channel_id=1, replica_groups=mesh['dp'=4,'fsdp'=8] {'fsdp'}, use_global_device_ids=true, to_apply=%add.7 | all-reduce | flops 9984 | bytes 39936
  772.7 10.0 %all-reduce.19 = (bf16[96]{0:T(256)(128)(2,1)S(1)}, bf16[96]{0:T(256)(128)(2,1)S(1)}, bf16[96]{0:T(256)(128)(2,1)S(1)}, bf16[96]{0:T(256)(128)(2,1)S(1)}, bf16[9...) all-reduce(bf16[96]{0:T(256)(128)(2,1)S(1)} %dynamic-slice.17, ...), channel_id=1, replica_groups=mesh['dp'=4,'fsdp'=8] {'dp'}, use_global_device_ids=true, to_apply=%region_47.48 | all-reduce | flops 1152 | bytes 4608 | tf_op jit(solution)/shard_map/psum | solution.py:366
  791.8 19.5 %all-reduce.23.cloned.1.call-done = (bf16[96,768]{1,0:T(8,128)(2,1)}, bf16[96,768]{1,0:T(8,128)(2,1)}, bf16[96,768]{1,0:T(8,128)(2,1)}, bf16[96,768]{1,0:T(8,128...) async-done(((bf16[96,768]{1,0:T(8,128)(2,1)}, bf16[96,768]{1,0:T(8,128)(2,1)}, bf16[96,768]{1,0:T(8,128)(2,1)}, bf16[96,768]{1,0:T(8,128)(2,1)}, ...) | async-done | bytes 1769488 | tf_op jit(solution)/shard_map/psum | solution.py:366
  (469 shorter events, 193.9 us)
Async XLA Ops:
  7.2 89.0 %copy-start.53 = (bf16[1024,768]{1,0:T(8,128)(2,1)S(1)}, bf16[1024,768]{1,0:T(8,128)(2,1)}, u32[]{:S(2)}) copy-start(bf16[1024,768]{1,0:T(8,128)(2,1)} %param.24) | copy-start | bytes 4718596
  7.2 97.6 %all-gather.7.cloned.1.call-start = ((), (), s32[]{:S(2)}) async-start(), calls=%async_computation.6 | async-start | bytes 1327104 | tf_op jit(solution)/shard_map/all_gather | solution.py:331
  7.9 100.4 %all-gather.9.cloned.1.call-start = ((), (), s32[]{:S(2)}) async-start(), calls=%async_computation.7 | async-start | bytes 1327104 | tf_op jit(solution)/shard_map/all_gather | solution.py:328
  8.7 102.8 %all-gather.11.cloned.1.call-start = ((), (), s32[]{:S(2)}) async-start(), calls=%async_computation.8 | async-start | bytes 1327104 | tf_op jit(solution)/shard_map/all_gather | solution.py:330
  9.4 159.4 %all-gather.13.cloned.1.call-start = ((), (), s32[]{:S(2)}) async-start(), calls=%async_computation.9 | async-start | bytes 1327104 | tf_op jit(solution)/shard_map/all_gather | solution.py:333
  9.5 2.4 collective-permute-start
  10.0 282.8 %all-gather.15.cloned.1.call-start = ((), (), s32[]{:S(2)}) async-start(), calls=%async_computation.10 | async-start | bytes 5308416 | tf_op jit(solution)/shard_map/all_gather | solution.py:339
  14.1 85.7 %collective-permute-start.1 = (bf16[2,96,3072]{2,1,0:T(8,128)(2,1)}, bf16[2,96,3072]{2,1,0:T(8,128)(2,1)}, u32[]{:S(2)}, u32[]{:S(2)}) collective-permute-start(bf16[2,96,3072]{2,1,0:T(8,128)(2,1)} %pad_maximum_fusion.4), channel_id=1, source_target_pairs={{0,2},{1,3},{2,0},{3,1},{4,6},{5,7},{6,4},{7,5},{8,10},{9,11},{10,... | collective-permute-start | bytes 3538952 | tf_op jit(solution)/shard_map/ppermute | solution.py:27
  17.1 513.7 %reduce-scatter.7.cloned.1.call-start = ((), (), s32[]{:S(2)}) async-start(), calls=%async_computation.11 | async-start | bytes 1327104 | tf_op jit(solution)/shard_map/reduce_scatter | solution.py:363
  103.9 149.1 %collective-permute-start.2 = (bf16[4,96,3072]{2,1,0:T(8,128)(2,1)}, bf16[4,96,3072]{2,1,0:T(8,128)(2,1)}, u32[]{:S(2)}, u32[]{:S(2)}) collective-permute-start(bf16[4,96,3072]{2,1,0:T(8,128)(2,1)} %pad_maximum_fusion.1), channel_id=1, source_target_pairs={{0,4},{1,5},{2,6},{3,7},{4,0},{5,1},{6,2},{7,3},{8,12},{9,13},{10,... | collective-permute-start | bytes 7077896 | tf_op jit(solution)/shard_map/ppermute | solution.py:27
  174.8 99.7 %copy-start.49 = (bf16[512,768]{1,0:T(8,128)(2,1)}, bf16[512,768]{1,0:T(8,128)(2,1)S(1)}, u32[]{:S(2)}) copy-start(bf16[512,768]{1,0:T(8,128)(2,1)S(1)} %get-tuple-element.894) | copy-start | bytes 2359300
  174.8 125.3 %copy-start.31 = (f32[512,768]{1,0:T(8,128)}, f32[512,768]{1,0:T(8,128)S(1)}, u32[]{:S(2)}) copy-start(f32[512,768]{1,0:T(8,128)S(1)} %get-tuple-element.895) | copy-start | bytes 4718596
  306.8 91.3 %copy-start.1 = (bf16[512,768]{0,1:T(8,128)(2,1)S(1)}, bf16[512,768]{0,1:T(8,128)(2,1)}, u32[]{:S(2)}) copy-start(bf16[512,768]{0,1:T(8,128)(2,1)} %copy-done) | copy-start | bytes 2359300
  306.8 91.3 %copy-start.61 = (f32[12,512]{1,0:T(8,128)S(1)}, f32[12,512]{1,0:T(8,128)}, u32[]{:S(2)}) copy-start(f32[12,512]{1,0:T(8,128)} %copy-done.60) | copy-start | bytes 73732
  306.8 91.3 %copy-start.65 = (f32[12,512]{1,0:T(8,128)S(1)}, f32[12,512]{1,0:T(8,128)}, u32[]{:S(2)}) copy-start(f32[12,512]{1,0:T(8,128)} %copy-done.64) | copy-start | bytes 73732
  306.8 91.3 %copy-start.91 = (f32[512]{0:T(512)S(1)}, f32[512]{0:T(512)}, u32[]{:S(2)}) copy-start(f32[512]{0:T(512)} %copy-done.90) | copy-start | bytes 6148
  498.9 66.2 %reduce-scatter.9.cloned.1.call-start = ((), (), s32[]{:S(2)}) async-start(), calls=%async_computation.12 | async-start | bytes 1327104 | tf_op jit(solution)/shard_map/reduce_scatter | solution.py:363
  501.6 97.5 %reduce-scatter.11.cloned.1.call-start = ((), (), s32[]{:S(2)}) async-start(), calls=%async_computation.13 | async-start | bytes 1327104 | tf_op jit(solution)/shard_map/reduce_scatter | solution.py:363
  504.4 128.9 %reduce-scatter.13.cloned.1.call-start = ((), (), s32[]{:S(2)}) async-start(), calls=%async_computation.14 | async-start | bytes 1327104 | tf_op jit(solution)/shard_map/reduce_scatter | solution.py:363
  507.2 181.4 %reduce-scatter.15.cloned.1.call-start = ((), (), s32[]{:S(2)}) async-start(), calls=%async_computation.15 | async-start | bytes 5308416 | tf_op jit(solution)/shard_map/reduce_scatter | solution.py:363
  515.0 229.3 %reduce-scatter.17.cloned.1.call-start = ((), (), s32[]{:S(2)}) async-start(), calls=%async_computation.16 | async-start | bytes 5308416 | tf_op jit(solution)/shard_map/reduce_scatter | solution.py:363
  522.7 222.9 %copy-start.110 = (bf16[96]{0:T(256)(128)(2,1)S(1)}, bf16[96]{0:T(256)(128)(2,1)}, u32[]{:S(2)}) copy-start(bf16[96]{0:T(256)(128)(2,1)} %param.41) | copy-start | bytes 580
  522.7 223.2 %copy-start.71 = (f32[768]{0:T(1024)S(1)}, f32[768]{0:T(1024)}, u32[]{:S(2)}) copy-start(f32[768]{0:T(1024)} %get-tuple-element.592) | copy-start | bytes 9220
  522.7 223.2 %copy-start.75 = (f32[768]{0:T(1024)S(1)}, f32[768]{0:T(1024)}, u32[]{:S(2)}) copy-start(f32[768]{0:T(1024)} %get-tuple-element.593) | copy-start | bytes 9220
  522.7 223.3 %copy-start.79 = (f32[768]{0:T(1024)S(1)}, f32[768]{0:T(1024)}, u32[]{:S(2)}) copy-start(f32[768]{0:T(1024)} %get-tuple-element.594) | copy-start | bytes 9220
  522.7 264.7 %copy-start.11 = (f32[512,768]{1,0:T(8,128)S(1)}, f32[512,768]{1,0:T(8,128)}, u32[]{:S(2)}) copy-start(f32[512,768]{1,0:T(8,128)} %copy-done.10) | copy-start | bytes 4718596
  522.7 264.7 %copy-start.13 = (f32[512,768]{1,0:T(8,128)S(1)}, f32[512,768]{1,0:T(8,128)}, u32[]{:S(2)}) copy-start(f32[512,768]{1,0:T(8,128)} %copy-done.12) | copy-start | bytes 4718596
  522.7 264.6 %copy-start.81 = (f32[512]{0:T(512)S(1)}, f32[512]{0:T(512)}, u32[]{:S(2)}) copy-start(f32[512]{0:T(512)} %copy-done.80) | copy-start | bytes 6148
  522.7 264.6 %copy-start.83 = (f32[512]{0:T(512)S(1)}, f32[512]{0:T(512)}, u32[]{:S(2)}) copy-start(f32[512]{0:T(512)} %copy-done.82) | copy-start | bytes 6148
  522.8 264.6 %copy-start.85 = (f32[512]{0:T(512)S(1)}, f32[512]{0:T(512)}, u32[]{:S(2)}) copy-start(f32[512]{0:T(512)} %copy-done.84) | copy-start | bytes 6148
  522.8 264.6 %copy-start.87 = (f32[512]{0:T(512)S(1)}, f32[512]{0:T(512)}, u32[]{:S(2)}) copy-start(f32[512]{0:T(512)} %copy-done.86) | copy-start | bytes 6148
  522.8 288.5 %all-reduce.23.cloned.1.call-start = ((), (), s32[]{:S(2)}) async-start(), calls=%async_computation.17 | async-start | bytes 3538944 | tf_op jit(solution)/shard_map/psum | solution.py:366
  (110 other events, 910.2 us)
Sparse Core Ops, SparseCore 0:
  9.6 31.6 all-gather.6
  43.0 24.6 all-gather.8
  69.3 22.5 all-gather.10
  93.3 75.4 all-gather.12
  170.3 70.1 all-gather.14
  499.0 31.7 reduce-scatter.6
  533.6 31.3 reduce-scatter.8
  567.9 31.1 reduce-scatter.10
  602.0 31.2 reduce-scatter.12
  635.4 53.1 reduce-scatter.14
  690.9 53.3 reduce-scatter.16
  747.9 63.3 all-reduce.22
